TPU v7x, 32 devices: a whole 2x2x4 slice. The times are simulated.
32 devices in a mesh: seq: 8 (over y, x, core), tp: 4 (over z).
Axes of the slice: x: 2, y: 2, z: 4, core: 2. Of those that a mesh axis runs over, the one named last changes fastest.
Arguments:
- states: bfloat16 [8, 128, 2048], P('seq', None, 'tp'), may hold values from -60 to 60, as said below
- cotangent: bfloat16 [8, 128, 2048], P('seq', None, 'tp'), may hold values from -12 to 12, as said below
- wq: bfloat16 [2048, 2048], P(None, 'tp'), may hold values from -0.125 to 0.125
- wk: bfloat16 [2048, 512], P(None, 'tp'), may hold values from -0.125 to 0.125
- wv: bfloat16 [2048, 512], P(None, 'tp'), may hold values from -0.125 to 0.125
- wo: bfloat16 [2048, 2048], P('tp'), may hold values from -0.125 to 0.125
Outputs:
- gram: float32 [8, 8], P('seq')
Inputs may be any that keep to these rules, and one draw needn't show every extreme that they name: `states`: finite values. `cotangent`: finite values.
All inputs are finite; a program needn't handle non-finite values.
Results may differ from a plain program's by a relative error of at most 0.0025.
Values may be sent and summed in bfloat16 or wider, within the bound.
A program may use at most 64 MiB of HBM per device.

v0:
```python
import jax
import jax.numpy as jnp
from jax import lax
from jax.sharding import PartitionSpec as P

HEADS = 32
KV_HEADS = 8
HEAD_DIM = 64
theta_base = 500000.0


def from_behind(block, axis, distance):
    devices = range(lax.axis_size(axis))
    route = [((i - distance) % len(devices), i) for i in devices]
    return lax.ppermute(block, axis, route)


def rope_tables(length, head_dim):
    half_dim = head_dim // 2
    freqs_k = theta_base ** (-(jnp.arange(half_dim, dtype=jnp.float32) * 2.0 / head_dim))
    angles = jnp.arange(length, dtype=jnp.float32)[:, None] * freqs_k[None, :]
    angles = jnp.concatenate([angles, angles], axis=1)
    return (jnp.cos(angles)[:, None, :], jnp.sin(angles)[:, None, :])


def rotate(values_in, cos_table, sine_table):
    half_dim = values_in.shape[-1] // 2
    turned = jnp.concatenate([-values_in[..., half_dim:], values_in[..., :half_dim]], axis=-1)
    return values_in * cos_table + turned * sine_table


def attention_factors(states, cotangent, wq, wk, wv, wo):
    seq_dev, length, part_width = states.shape
    full_states, full_cot = (
        lax.all_gather(states, "tp", axis=2, tiled=True),
        lax.all_gather(cotangent, "tp", axis=2, tiled=True),
    )
    model_width = full_states.shape[2]
    tok_rows = seq_dev * length
    kv_local = wk.shape[1] // HEAD_DIM
    group_size = HEADS // KV_HEADS
    cos_table, sine_table = rope_tables(length, HEAD_DIM)
    flat_states = full_states.reshape(tok_rows, model_width)
    query_heads = jnp.dot(flat_states, wq, preferred_element_type=jnp.float32).reshape(
        seq_dev, length, kv_local * group_size, HEAD_DIM
    )
    query_heads = (
        rotate(query_heads, cos_table, sine_table)
        .astype(jnp.bfloat16)
        .reshape(seq_dev, length, kv_local, group_size, HEAD_DIM)
    )
    key_heads = jnp.dot(flat_states, wk, preferred_element_type=jnp.float32).reshape(
        seq_dev, length, kv_local, HEAD_DIM
    )
    key_heads = rotate(key_heads, cos_table, sine_table).astype(jnp.bfloat16)
    value_heads = (
        jnp.dot(flat_states, wv, preferred_element_type=jnp.float32)
        .astype(jnp.bfloat16)
        .reshape(seq_dev, length, kv_local, HEAD_DIM)
    )
    scores = jnp.einsum(
        "sqkgd,stkd->skgqt", query_heads, key_heads, preferred_element_type=jnp.float32
    ) * HEAD_DIM ** (-0.5)
    causal = jnp.arange(length)[:, None] >= jnp.arange(length)[None, :]
    scores = jnp.where(causal, scores, -jnp.inf)
    weights_bf = jax.nn.softmax(scores, axis=-1).astype(jnp.bfloat16)
    attended = (
        jnp.einsum("skgqt,stkd->sqkgd", weights_bf, value_heads, preferred_element_type=jnp.float32)
        .astype(jnp.bfloat16)
        .reshape(tok_rows, part_width)
    )
    grad_attended = (
        lax.dot_general(
            full_cot.reshape(tok_rows, model_width),
            wo,
            (((1,), (1,)), ((), ())),
            preferred_element_type=jnp.float32,
        )
        .astype(jnp.bfloat16)
        .reshape(seq_dev, length, kv_local, group_size, HEAD_DIM)
    )
    value_gradient = (
        jnp.einsum(
            "skgqt,sqkgd->stkd", weights_bf, grad_attended, preferred_element_type=jnp.float32
        )
        .astype(jnp.bfloat16)
        .reshape(tok_rows, kv_local * HEAD_DIM)
    )
    return jnp.concatenate(
        [
            states.reshape(tok_rows, part_width),
            attended,
            cotangent.reshape(tok_rows, part_width),
            value_gradient,
        ],
        axis=1,
    )


def tile_of(left_rows, right_rows, begin_col, end_col):
    return lax.dot_general(
        left_rows[:, begin_col:end_col],
        right_rows[:, begin_col:end_col],
        (((1,), (1,)), ((), ())),
        preferred_element_type=jnp.float32,
    )


def pair_block(own_rows, other_rows, part_width, seq_dev, length):
    tiles = jnp.stack(
        [
            tile_of(own_rows, other_rows, 0, part_width),
            tile_of(own_rows, other_rows, part_width, 2 * part_width),
            tile_of(own_rows, other_rows, 2 * part_width, 3 * part_width),
            tile_of(own_rows, other_rows, 3 * part_width, own_rows.shape[1]),
        ]
    )
    shares = lax.psum_scatter(
        tiles.astype(jnp.bfloat16), "tp", scatter_dimension=1, tiled=True
    ).astype(jnp.float32)
    product = shares[0] * shares[3] + shares[1] * shares[2]
    share_rows = product.shape[0]
    col_sums = product.reshape(share_rows, seq_dev, length).sum(axis=2)
    first_row = lax.axis_index("tp") * share_rows
    row_seq = (first_row + jnp.arange(share_rows, dtype=jnp.int32)) // length
    member = (row_seq[None, :] == jnp.arange(seq_dev, dtype=jnp.int32)[:, None]).astype(jnp.float32)
    return jnp.dot(member, col_sums, precision=lax.Precision.HIGHEST)


def record(totals, block, distance, me_index, n_seq, half_rotation):
    row_acc, col_acc = totals
    seq_dev = block.shape[0]
    distance = jnp.asarray(distance, jnp.int32)
    offset = (me_index + distance) % n_seq * seq_dev
    zero_at = jnp.zeros((), jnp.int32)
    row_on = jnp.where(distance < half_rotation, 1.0, 0.0).astype(jnp.float32)
    row_acc = lax.dynamic_update_slice(row_acc, block * row_on, (zero_at, offset))
    mirror_on = jnp.where((distance > 0) & (distance <= half_rotation), 1.0, 0.0).astype(
        jnp.float32
    )
    col_acc = lax.dynamic_update_slice(col_acc, block.T * mirror_on, (offset, zero_at))
    return (row_acc, col_acc)


def on_device(states, cotangent, wq, wk, wv, wo):
    seq_dev, length, part_width = states.shape
    own_rows = attention_factors(states, cotangent, wq, wk, wv, wo)
    n_seq = lax.axis_size("seq")
    half_rotation = n_seq // 2
    me_index = lax.axis_index("seq")
    totals = (
        jnp.zeros((seq_dev, n_seq * seq_dev), jnp.float32),
        jnp.zeros((n_seq * seq_dev, seq_dev), jnp.float32),
    )

    def measure(totals_in, other_rows, distance):
        block = pair_block(own_rows, other_rows, part_width, seq_dev, length)
        return record(totals_in, block, distance, me_index, n_seq, half_rotation)

    totals = measure(totals, own_rows, 0)
    near_count = half_rotation // 2
    far_count = half_rotation - 1 - near_count
    opposite = from_behind(own_rows, "seq", half_rotation)
    totals = measure(totals, opposite, half_rotation)

    def near_turn(visitor, totals_in, distance):
        visitor = from_behind(visitor, "seq", -1)
        return (visitor, measure(totals_in, visitor, distance))

    def paired_turn(step_index, carried):
        near_rows, far_rows, totals_in = carried
        near_rows, totals_in = near_turn(near_rows, totals_in, step_index + 1)
        far_rows = from_behind(far_rows, "seq", 1)
        return (near_rows, far_rows, measure(totals_in, far_rows, half_rotation - 1 - step_index))

    near_rows, far_rows, totals = lax.fori_loop(
        0, far_count, paired_turn, (own_rows, opposite, totals)
    )
    near_rows, totals = near_turn(near_rows, totals, near_count)
    row_acc, col_acc = lax.psum((totals[0], totals[1]), "tp")
    mirrored = lax.all_to_all(col_acc, "seq", split_axis=0, concat_axis=1, tiled=True)
    kernel = row_acc + mirrored
    own_block = lax.dynamic_slice_in_dim(kernel, me_index * seq_dev, seq_dev, 1)
    own_diag = jnp.diagonal(own_block)
    all_diag = lax.all_gather(own_diag, "seq", axis=0, tiled=True)
    return kernel / jnp.sqrt(own_diag[:, None] * all_diag[None, :])


def solution(mesh):
    in_specs = (
        P("seq", None, "tp"),
        P("seq", None, "tp"),
        P(None, "tp"),
        P(None, "tp"),
        P(None, "tp"),
        P("tp", None),
    )
    out_specs = P("seq", None)
    return jax.shard_map(
        on_device, mesh=mesh, in_specs=in_specs, out_specs=out_specs, check_vma=False
    )
```

profile of v0, /device:TPU:0, one launch (start us, length us, event | category | flops | bytes accessed | tf_op | source)
XLA Modules:
  0.0 167.4 jit_solution(4516252075770573431)
XLA Ops:
  6.7 17.7 %all_gather.9 = bf16[1,128,2048]{2,1,0:T(8,128)(2,1)S(1)} all-gather(bf16[1,128,512]{2,1,0:T(8,128)(2,1)} %param.6), channel_id=1, replica_groups=mesh['seq'=8,'tp'=4] {'tp'}, dimensions={2}, use_global_device_ids=true | all-gather | bytes 655360 | tf_op jit(solution)/shard_map/all_gather | solution.py:35
  24.4 1.4 convolution_convert_fusion.19
  25.8 1.4 fusion.28
  27.2 0.9 fusion.26
  28.3 0.3 fusion.88
  28.8 0.2 convolution_convert_fusion.1
  29.1 16.4 %all_gather.10 = bf16[1,128,2048]{2,1,0:T(8,128)(2,1)S(1)} all-gather(bf16[1,128,512]{2,1,0:T(8,128)(2,1)S(1)} %copy-done.1), channel_id=1, replica_groups=mesh['seq'=8,'tp'=4] {'tp'}, dimensions={2}, use_global_device_ids=true | all-gather | bytes 655360 | tf_op jit(solution)/shard_map/all_gather | solution.py:36
  45.5 2.4 %convolution_convert_fusion = bf16[128,512]{1,0:T(8,128)(2,1)S(1)} fusion(bf16[512,2048]{1,0:T(8,128)(2,1)} %param.11, bf16[1,128,2048]{2,1,0:T(8,128)(2,1)S(1)} %all_gather.10), kind=kOutput, calls=%fused_computation.3 | convolution fusion | flops 268500992 | bytes 2752512 | tf_op jit(solution)/shard_map/dot_general | solution.py:73
  48.0 0.2 fusion.2
  48.5 1.6 collective-permute-start
  50.1 0.2 fusion.5
  50.3 0.2 fusion.23
  50.4 0.2 fusion.6
  50.6 0.2 fusion.24
  50.9 0.7 pad_maximum_fusion.1
  51.6 2.6 %collective-permute-done.1 = bf16[128,1664]{1,0:T(8,128)(2,1)} collective-permute-done((bf16[128,1664]{1,0:T(8,128)(2,1)S(1)}, bf16[128,1664]{1,0:T(8,128)(2,1)}, u32[]{:S(2)}, u32[]{:S(2)}) %collective-permute-start.1) | collective-permute-done | bytes 426016 | tf_op jit(solution)/shard_map/while/body/eval_jaxpr/ppermute | solution.py:15
  54.2 1.1 fusion.10
  55.3 0.9 fusion.18
  56.2 1.1 fusion.17
  57.2 1.1 fusion.9
  58.4 0.8 copy.71
  59.2 3.0 %collective-permute-start.3 = (bf16[128,1664]{1,0:T(8,128)(2,1)}, bf16[128,1664]{1,0:T(8,128)(2,1)}, u32[]{:S(2)}, u32[]{:S(2)}) collective-permute-start(bf16[128,1664]{1,0:T(8,128)(2,1)} %collective-permute-done.1), channel_id=1, source_target_pairs={{4,0},{8,4},{12,8},{16,12},{20,16},{24,20},{28,24},{0,28},{5,1},{9... | collective-permute-start | bytes 1277960 | tf_op jit(solution)/shard_map/ppermute | solution.py:15
  62.1 0.2 fusion.8
  62.4 0.2 fusion.15
  62.6 0.2 fusion.7
  62.9 0.8 copy.68
  63.7 4.4 %collective-permute-done.3 = bf16[128,1664]{1,0:T(8,128)(2,1)} collective-permute-done((bf16[128,1664]{1,0:T(8,128)(2,1)}, bf16[128,1664]{1,0:T(8,128)(2,1)}, u32[]{:S(2)}, u32[]{:S(2)}) %collective-permute-start.3) | collective-permute-done | bytes 426016 | tf_op jit(solution)/shard_map/ppermute | solution.py:15
  68.1 1.1 fusion.14
  69.2 0.9 fusion.22
  70.1 1.1 fusion.21
  71.2 1.1 fusion.13
  72.3 2.3 %collective-permute-done.2 = bf16[128,1664]{1,0:T(8,128)(2,1)S(1)} collective-permute-done((bf16[128,1664]{1,0:T(8,128)(2,1)S(1)}, bf16[128,1664]{1,0:T(8,128)(2,1)S(1)}, u32[]{:S(2)}, u32[]{:S(2)}) %collective-permute-start.2) | collective-permute-done | bytes 426016 | tf_op jit(solution)/shard_map/while/body/eval_jaxpr/ppermute | solution.py:15
  74.8 0.2 fusion.12
  75.1 0.8 copy.77
  75.9 0.2 fusion.11
  76.1 0.8 copy.74
  77.0 0.6 dynamic-slice.1
  78.3 0.8 convert_element_type.81
  79.2 0.6 select_reduce_fusion.4
  80.5 0.7 dynamic_update_slice.34
  81.2 34.0 %all-reduce.9.cloned.1.call-done = (bf16[4,128,128]{2,0,1:T(4,128)(2,1)}, bf16[4,128,128]{2,0,1:T(4,128)(2,1)}, bf16[4,128,128]{2,0,1:T(4,128)(2,1)}, bf16[4,128,128]{2,0,1:T(4,128)(2,1)}) async-done(((bf16[4,128,128]{2,0,1:T(4,128)(2,1)}, bf16[4,128,128]{2,0,1:T(4,128)(2,1)}, bf16[4,128,128]{2,0,1:T(4,128)(2,1)}, bf16[4,128,128]{2,0,1:T(4,128)(2,1)}), (bf16[4,128,128]{2,0,1:T(4,128)(2,1)}, ...) | async-done | bytes 524304
  115.2 0.8 dynamic-slice_convert_fusion.3
  116.0 0.3 fusion.72
  116.3 0.8 dynamic-slice_convert_fusion.2
  117.1 0.3 fusion.73
  117.4 0.7 select_reduce_fusion.2
  118.7 0.8 dynamic-slice_convert_fusion.1
  119.5 0.8 dynamic-slice_convert_fusion
  120.3 0.3 fusion.75
  120.6 0.3 fusion.74
  121.0 0.6 constant_dynamic-update-slice_fusion.3
  121.7 0.7 constant_dynamic-update-slice_fusion.2
  122.3 0.8 dynamic_update_slice.36
  123.1 0.7 select_reduce_fusion
  123.8 0.8 dynamic_update_slice.37
  124.6 0.7 constant_dynamic-update-slice_fusion.1
  125.3 0.7 constant_dynamic-update-slice_fusion
  125.9 0.8 dynamic_update_slice.38
  126.7 0.6 dynamic-slice
  127.3 10.7 %all-reduce.5 = (f32[1,8]{1,0:T(1,128)S(1)}, f32[8,1,1]{2,1,0:T(1,128)S(1)}) all-reduce(f32[1,8]{1,0:T(1,128)S(1)} %dynamic_update_slice.38, f32[8,1,1]{2,1,0:T(1,128)S(1)} %constant_dynamic-update-slice_fusion), channel_id=1, replica_groups=mesh['seq'=8,'tp'=4] {'tp'}, use_global_device_ids=true, to_apply=%region_12.13 | all-reduce | flops 16 | bytes 128 | tf_op jit(solution)/shard_map/psum | solution.py:180
  138.0 8.1 %all_to_all.16 = f32[8,1,1]{2,1,0:T(1,128)S(1)} all-to-all(f32[8,1,1]{2,1,0:T(1,128)S(1)} %get-tuple-element.26), channel_id=1, replica_groups=mesh['seq'=8,'tp'=4] {'seq'}, dimensions={0} | all-to-all | bytes 64 | tf_op jit(solution)/shard_map/all_to_all | solution.py:181
  146.2 1.3 bitcast_dynamic-update-slice_fusion
  147.5 11.8 %all-reduce = f32[8]{0:T(128)S(1)} all-reduce(f32[8]{0:T(128)S(1)} %get-tuple-element.52), channel_id=2, replica_groups=mesh['seq'=8,'tp'=4] {'seq'}, use_global_device_ids=true, to_apply=%add | all-reduce | flops 8 | bytes 64
  159.3 1.2 bitcast_multiply_fusion
  (45 shorter events, 1.9 us)
Async XLA Ops:
  6.5 20.7 %copy-start = (bf16[2048,512]{1,0:T(8,128)(2,1)S(1)}, bf16[2048,512]{1,0:T(8,128)(2,1)}, u32[]{:S(2)}) copy-start(bf16[2048,512]{1,0:T(8,128)(2,1)} %param.8) | copy-start | bytes 6291460
  6.5 71.8 %reduce-scatter.2.cloned.1.call-start = ((), (), s32[]{:S(2)}) async-start(), calls=%async_computation.2 | async-start | bytes 163840 | tf_op jit(solution)/shard_map/reduce_scatter | solution.py:118
  28.2 0.9 copy-start.1
  29.1 19.3 %copy-start.2 = (bf16[1,128,512]{2,1,0:T(8,128)(2,1)S(1)}, bf16[1,128,512]{2,1,0:T(8,128)(2,1)}, u32[]{:S(2)}) copy-start(bf16[1,128,512]{2,1,0:T(8,128)(2,1)} %param.6) | copy-start | bytes 393220
  48.4 5.7 %collective-permute-start.1 = (bf16[128,1664]{1,0:T(8,128)(2,1)S(1)}, bf16[128,1664]{1,0:T(8,128)(2,1)}, u32[]{:S(2)}, u32[]{:S(2)}) collective-permute-start(bf16[128,1664]{1,0:T(8,128)(2,1)S(1)} %pad_maximum_fusion), channel_id=1, source_target_pairs={{4,0},{8,4},{12,8},{16,12},{20,16},{24,20},{28,24},{0,28},{5,1},{9... | collective-permute-start | bytes 1277960 | tf_op jit(solution)/shard_map/while/body/eval_jaxpr/ppermute | solution.py:15
  48.5 13.6 %collective-permute-start = (bf16[128,1664]{1,0:T(8,128)(2,1)S(1)}, bf16[128,1664]{1,0:T(8,128)(2,1)S(1)}, u32[]{:S(2)}, u32[]{:S(2)}) collective-permute-start(bf16[128,1664]{1,0:T(8,128)(2,1)S(1)} %pad_maximum_fusion), channel_id=1, source_target_pairs={{16,0},{20,4},{24,8},{28,12},{0,16},{4,20},{8,24},{12,28},{17,1},{... | collective-permute-start | bytes 1277960 | tf_op jit(solution)/shard_map/ppermute | solution.py:15
  51.6 63.7 %all-reduce.9.cloned.1.call-start = ((), (), s32[]{:S(2)}) async-start(), calls=%async_computation.3 | async-start | bytes 1048576
  59.2 8.9 %collective-permute-start.3 = (bf16[128,1664]{1,0:T(8,128)(2,1)}, bf16[128,1664]{1,0:T(8,128)(2,1)}, u32[]{:S(2)}, u32[]{:S(2)}) collective-permute-start(bf16[128,1664]{1,0:T(8,128)(2,1)} %collective-permute-done.1), channel_id=1, source_target_pairs={{4,0},{8,4},{12,8},{16,12},{20,16},{24,20},{28,24},{0,28},{5,1},{9... | collective-permute-start | bytes 1277960 | tf_op jit(solution)/shard_map/ppermute | solution.py:15
  62.8 14.2 %copy-start.4 = (u32[32]{0:T(128)S(1)}, u32[32]{0:T(128)}, u32[]{:S(2)}) copy-start(u32[32]{0:T(128)} %constant.159) | copy-start | bytes 388
  63.7 11.0 %collective-permute-start.2 = (bf16[128,1664]{1,0:T(8,128)(2,1)S(1)}, bf16[128,1664]{1,0:T(8,128)(2,1)S(1)}, u32[]{:S(2)}, u32[]{:S(2)}) collective-permute-start(bf16[128,1664]{1,0:T(8,128)(2,1)S(1)} %collective-permute-done), channel_id=1, source_target_pairs={{28,0},{0,4},{4,8},{8,12},{12,16},{16,20},{20,24},{24,28},{29,1},{... | collective-permute-start | bytes 1277960 | tf_op jit(solution)/shard_map/while/body/eval_jaxpr/ppermute | solution.py:15
  70.1 56.6 %copy-start.3 = (u32[32]{0:T(128)S(1)}, u32[32]{0:T(128)}, u32[]{:S(2)}) copy-start(u32[32]{0:T(128)} %constant.143) | copy-start | bytes 388
Sparse Core Ops, SparseCore 0:
  51.7 18.9 reduce-scatter.1
  77.1 38.1 all-reduce.8
where the time goes:
time: 168 us; the launch traced here: 167 us
  blocking collectives  64.7 us (39%)
  waiting for transfers between devices  43.4 us (26%)
  matrix products  17.2 us (10%)
  between operations  15.8 us (9%)
  local copies, waits for them, and re-layouts  11.8 us (7%)
  other arithmetic  9.77 us (6%)
  starting transfers between devices  4.64 us (3%)
    unnamed x3, waiting for transfers between devices  34.1 us
    all_gather x1, blocking collectives, attention_factors(): lax.all_gather(states, 'tp', axis=2, tiled=True)  17.7 us
    all_gather x1, blocking collectives, attention_factors(): lax.all_gather(cotangent, 'tp', axis=2, tiled=True)  16.4 us
    unnamed x1, blocking collectives  11.8 us
    psum x1, blocking collectives, on_device(): row_acc, col_acc = lax.psum((totals[0], totals[1]), 'tp')  10.7 us
    dot_general x20, matrix products, tile_of(): lax.dot_general(left_rows[:, begin_col:end_col], right_rows[:, begin_col:...  10.4 us
    ppermute x4, waiting for transfers between devices, from_behind(): return lax.ppermute(block, axis, route)  9.32 us
    all_to_all x1, blocking collectives, on_device(): lax.all_to_all(col_acc, 'seq', split_axis=0, concat_axis=1, tiled=True)  8.08 us
  transfers between devices with their start and end apart: 6, of which 4 were waited for; matrix products, arithmetic and copies ran while one was open for 10% of the time, Pallas kernels for 0%

commit v1 on v0

--- a/solution.py
+++ b/solution.py
@@ -32,7 +32,7 @@
 def attention_factors(states, cotangent, wq, wk, wv, wo):
     seq_dev, length, part_width = states.shape
     full_states, full_cot = (
-        lax.all_gather(states, "tp", axis=2, tiled=True),
+        jnp.concatenate(lax.all_gather(states, "tp"), axis=2),
         lax.all_gather(cotangent, "tp", axis=2, tiled=True),
     )
     model_width = full_states.shape[2]

time: 168 us -> 175 us (1.042)
  waiting for transfers between devices: 43.4 us -> 51.8 us
  matrix products: 17.2 us -> 14.7 us
    ppermute x4, waiting for transfers between devices: 9.32 us -> 17 us  [from_behind(): return lax.ppermute(block, axis, route)]
    dot_general x20, matrix products: 10.4 us -> 7.87 us  [tile_of(): lax.dot_general(left_rows[:, begin_col:end_col], right_rows[:, begin_col:...]
  transfers between devices with their start and end apart: 6 -> 6, of which waited for: 4 -> 5; matrix products, arithmetic and copies ran while one was open for 10% -> 8% of each run, Pallas kernels for 0% -> 0%
where the time goes in v1:
time: 175 us; the launch traced here: 174 us
  blocking collectives  64.7 us (37%)
  waiting for transfers between devices  51.8 us (30%)
  between operations  15.8 us (9%)
  matrix products  14.7 us (8%)
  local copies, waits for them, and re-layouts  12.5 us (7%)
  other arithmetic  10.5 us (6%)
  starting transfers between devices  4.32 us (2%)
    unnamed x3, waiting for transfers between devices  34.9 us
    all_gather x1, blocking collectives, attention_factors(): lax.all_gather(states, 'tp')  17.7 us
    ppermute x4, waiting for transfers between devices, from_behind(): return lax.ppermute(block, axis, route)  17 us
    all_gather x1, blocking collectives, attention_factors(): lax.all_gather(cotangent, 'tp', axis=2, tiled=True)  16.4 us
    unnamed x1, blocking collectives  11.8 us
    psum x1, blocking collectives, on_device(): row_acc, col_acc = lax.psum((totals[0], totals[1]), 'tp')  10.7 us
    all_to_all x1, blocking collectives, on_device(): lax.all_to_all(col_acc, 'seq', split_axis=0, concat_axis=1, tiled=True)  8.08 us
    dot_general x20, matrix products, tile_of(): lax.dot_general(left_rows[:, begin_col:end_col], right_rows[:, begin_col:...  7.87 us
  transfers between devices with their start and end apart: 6, of which 5 were waited for; matrix products, arithmetic and copies ran while one was open for 8% of the time, Pallas kernels for 0%

profile of v1, /device:TPU:0, one launch (start us, length us, event | category | flops | bytes accessed | tf_op | source)
XLA Modules:
  0.0 174.3 jit_solution(13683749775748066529)
XLA Ops:
  6.7 17.7 %all-gather = bf16[4,128,512]{2,1,0:T(8,128)(2,1)S(1)} all-gather(bf16[1,128,512]{2,1,0:T(8,128)(2,1)} %param.6), channel_id=2, replica_groups=mesh['seq'=8,'tp'=4] {'tp'}, dimensions={0}, use_global_device_ids=true | all-gather | bytes 655360 | tf_op jit(solution)/shard_map/all_gather | solution.py:35
  24.4 0.3 copy.61
  24.7 1.4 convolution_convert_fusion.19
  26.1 1.4 fusion.84
  27.5 0.9 fusion.85
  28.5 0.3 fusion.83
  29.4 16.4 %all_gather.14 = bf16[1,128,2048]{2,1,0:T(8,128)(2,1)S(1)} all-gather(bf16[1,128,512]{2,1,0:T(8,128)(2,1)S(1)} %copy-done.1), channel_id=1, replica_groups=mesh['seq'=8,'tp'=4] {'tp'}, dimensions={2}, use_global_device_ids=true | all-gather | bytes 655360 | tf_op jit(solution)/shard_map/all_gather | solution.py:36
  45.7 2.4 %convolution_convert_fusion = bf16[128,512]{1,0:T(8,128)(2,1)S(1)} fusion(bf16[512,2048]{1,0:T(8,128)(2,1)} %param.11, bf16[1,128,2048]{2,1,0:T(8,128)(2,1)S(1)} %all_gather.14), kind=kOutput, calls=%fused_computation.3 | convolution fusion | flops 268500992 | bytes 2752512 | tf_op jit(solution)/shard_map/dot_general | solution.py:73
  48.3 0.2 fusion.2
  48.6 0.8 pad_maximum_fusion
  49.4 1.5 collective-permute-start
  50.9 0.2 fusion.5
  51.1 0.2 fusion.23
  51.3 0.2 fusion.6
  51.5 0.2 fusion.24
  51.7 0.7 pad_maximum_fusion.1
  52.5 2.9 %collective-permute-done.1 = bf16[128,1664]{1,0:T(8,128)(2,1)S(1)} collective-permute-done((bf16[128,1664]{1,0:T(8,128)(2,1)}, bf16[128,1664]{1,0:T(8,128)(2,1)S(1)}, u32[]{:S(2)}, u32[]{:S(2)}) %collective-permute-start.1) | collective-permute-done | bytes 426016 | tf_op jit(solution)/shard_map/while/body/eval_jaxpr/ppermute | solution.py:15
  55.7 0.2 fusion.17
  55.9 0.2 fusion.9
  56.2 0.8 copy.74
  56.9 2.8 %collective-permute-start.3 = (bf16[128,1664]{1,0:T(8,128)(2,1)S(1)}, bf16[128,1664]{1,0:T(8,128)(2,1)}, u32[]{:S(2)}, u32[]{:S(2)}) collective-permute-start(bf16[128,1664]{1,0:T(8,128)(2,1)S(1)} %collective-permute-done.1), channel_id=1, source_target_pairs={{4,0},{8,4},{12,8},{16,12},{20,16},{24,20},{28,24},{0,28},{5,1},{9... | collective-permute-start | bytes 1277960 | tf_op jit(solution)/shard_map/ppermute | solution.py:15
  59.7 2.2 %collective-permute-done = bf16[128,1664]{1,0:T(8,128)(2,1)S(1)} collective-permute-done((bf16[128,1664]{1,0:T(8,128)(2,1)}, bf16[128,1664]{1,0:T(8,128)(2,1)S(1)}, u32[]{:S(2)}, u32[]{:S(2)}) %collective-permute-start) | collective-permute-done | bytes 426016 | tf_op jit(solution)/shard_map/ppermute | solution.py:15
  62.2 0.2 fusion.15
  62.4 0.2 fusion.7
  62.6 0.8 copy.71
  63.4 2.0 %collective-permute-done.3 = bf16[128,1664]{1,0:T(8,128)(2,1)} collective-permute-done((bf16[128,1664]{1,0:T(8,128)(2,1)S(1)}, bf16[128,1664]{1,0:T(8,128)(2,1)}, u32[]{:S(2)}, u32[]{:S(2)}) %collective-permute-start.3) | collective-permute-done | bytes 426016 | tf_op jit(solution)/shard_map/ppermute | solution.py:15
  65.4 1.1 fusion.14
  66.5 0.9 fusion.22
  67.4 1.1 fusion.21
  68.5 1.1 fusion.13
  69.6 9.9 %collective-permute-done.2 = bf16[128,1664]{1,0:T(8,128)(2,1)S(1)} collective-permute-done((bf16[128,1664]{1,0:T(8,128)(2,1)S(1)}, bf16[128,1664]{1,0:T(8,128)(2,1)S(1)}, u32[]{:S(2)}, u32[]{:S(2)}) %collective-permute-start.2) | collective-permute-done | bytes 426016 | tf_op jit(solution)/shard_map/while/body/eval_jaxpr/ppermute | solution.py:15
  79.6 0.2 fusion.12
  79.8 0.4 copy-done.3
  80.3 0.8 copy.80
  81.1 1.1 fusion.11
  82.3 0.8 copy.77
  83.1 0.6 dynamic-slice.1
  84.4 0.8 convert_element_type.81
  85.3 0.6 select_reduce_fusion.4
  86.6 0.7 dynamic_update_slice.34
  87.3 34.8 %all-reduce.9.cloned.1.call-done = (bf16[4,128,128]{2,0,1:T(4,128)(2,1)}, bf16[4,128,128]{2,0,1:T(4,128)(2,1)}, bf16[4,128,128]{2,0,1:T(4,128)(2,1)}, bf16[4,128,128]{2,0,1:T(4,128)(2,1)}) async-done(((bf16[4,128,128]{2,0,1:T(4,128)(2,1)}, bf16[4,128,128]{2,0,1:T(4,128)(2,1)}, bf16[4,128,128]{2,0,1:T(4,128)(2,1)}, bf16[4,128,128]{2,0,1:T(4,128)(2,1)}), (bf16[4,128,128]{2,0,1:T(4,128)(2,1)}, ...) | async-done | bytes 524304
  122.2 0.8 dynamic-slice_convert_fusion.3
  122.9 0.3 fusion.67
  123.2 0.8 dynamic-slice_convert_fusion.2
  124.0 0.3 fusion.68
  124.3 0.7 select_reduce_fusion.2
  125.6 0.8 dynamic-slice_convert_fusion.1
  126.4 0.8 dynamic-slice_convert_fusion
  127.2 0.3 fusion.70
  127.5 0.3 fusion.69
  127.9 0.6 constant_dynamic-update-slice_fusion.3
  128.6 0.7 constant_dynamic-update-slice_fusion.2
  129.2 0.8 dynamic_update_slice.36
  130.0 0.7 select_reduce_fusion
  130.7 0.8 dynamic_update_slice.37
  131.5 0.7 constant_dynamic-update-slice_fusion.1
  132.2 0.7 constant_dynamic-update-slice_fusion
  132.9 0.8 dynamic_update_slice.38
  133.6 0.6 dynamic-slice
  134.2 10.7 %all-reduce.5 = (f32[1,8]{1,0:T(1,128)S(1)}, f32[8,1,1]{2,1,0:T(1,128)S(1)}) all-reduce(f32[1,8]{1,0:T(1,128)S(1)} %dynamic_update_slice.38, f32[8,1,1]{2,1,0:T(1,128)S(1)} %constant_dynamic-update-slice_fusion), channel_id=1, replica_groups=mesh['seq'=8,'tp'=4] {'tp'}, use_global_device_ids=true, to_apply=%region_12.13 | all-reduce | flops 16 | bytes 128 | tf_op jit(solution)/shard_map/psum | solution.py:180
  144.9 8.1 %all_to_all.16 = f32[8,1,1]{2,1,0:T(1,128)S(1)} all-to-all(f32[8,1,1]{2,1,0:T(1,128)S(1)} %get-tuple-element.26), channel_id=1, replica_groups=mesh['seq'=8,'tp'=4] {'seq'}, dimensions={0} | all-to-all | bytes 64 | tf_op jit(solution)/shard_map/all_to_all | solution.py:181
  153.1 1.3 bitcast_dynamic-update-slice_fusion
  154.5 11.8 %all-reduce = f32[8]{0:T(128)S(1)} all-reduce(f32[8]{0:T(128)S(1)} %get-tuple-element.52), channel_id=3, replica_groups=mesh['seq'=8,'tp'=4] {'seq'}, use_global_device_ids=true, to_apply=%add | all-reduce | flops 8 | bytes 64
  166.3 1.2 bitcast_multiply_fusion
  (48 shorter events, 2.5 us)
Async XLA Ops:
  6.5 21.0 %copy-start = (bf16[2048,512]{1,0:T(8,128)(2,1)S(1)}, bf16[2048,512]{1,0:T(8,128)(2,1)}, u32[]{:S(2)}) copy-start(bf16[2048,512]{1,0:T(8,128)(2,1)} %param.8) | copy-start | bytes 6291460
  6.5 77.9 %reduce-scatter.2.cloned.1.call-start = ((), (), s32[]{:S(2)}) async-start(), calls=%async_computation.2 | async-start | bytes 163840 | tf_op jit(solution)/shard_map/reduce_scatter | solution.py:118
  28.4 0.9 copy-start.1
  29.4 19.3 %copy-start.2 = (bf16[1,128,512]{2,1,0:T(8,128)(2,1)S(1)}, bf16[1,128,512]{2,1,0:T(8,128)(2,1)}, u32[]{:S(2)}) copy-start(bf16[1,128,512]{2,1,0:T(8,128)(2,1)} %param.6) | copy-start | bytes 393220
  49.4 6.0 %collective-permute-start.1 = (bf16[128,1664]{1,0:T(8,128)(2,1)}, bf16[128,1664]{1,0:T(8,128)(2,1)S(1)}, u32[]{:S(2)}, u32[]{:S(2)}) collective-permute-start(bf16[128,1664]{1,0:T(8,128)(2,1)} %pad_maximum_fusion), channel_id=1, source_target_pairs={{4,0},{8,4},{12,8},{16,12},{20,16},{24,20},{28,24},{0,28},{5,1},{9... | collective-permute-start | bytes 1277960 | tf_op jit(solution)/shard_map/while/body/eval_jaxpr/ppermute | solution.py:15
  49.4 12.4 %collective-permute-start = (bf16[128,1664]{1,0:T(8,128)(2,1)}, bf16[128,1664]{1,0:T(8,128)(2,1)S(1)}, u32[]{:S(2)}, u32[]{:S(2)}) collective-permute-start(bf16[128,1664]{1,0:T(8,128)(2,1)} %pad_maximum_fusion), channel_id=1, source_target_pairs={{16,0},{20,4},{24,8},{28,12},{0,16},{4,20},{8,24},{12,28},{17,1},{... | collective-permute-start | bytes 1277960 | tf_op jit(solution)/shard_map/ppermute | solution.py:15
  52.4 69.7 %all-reduce.9.cloned.1.call-start = ((), (), s32[]{:S(2)}) async-start(), calls=%async_computation.3 | async-start | bytes 1048576
  56.9 8.4 %collective-permute-start.3 = (bf16[128,1664]{1,0:T(8,128)(2,1)S(1)}, bf16[128,1664]{1,0:T(8,128)(2,1)}, u32[]{:S(2)}, u32[]{:S(2)}) collective-permute-start(bf16[128,1664]{1,0:T(8,128)(2,1)S(1)} %collective-permute-done.1), channel_id=1, source_target_pairs={{4,0},{8,4},{12,8},{16,12},{20,16},{24,20},{28,24},{0,28},{5,1},{9... | collective-permute-start | bytes 1277960 | tf_op jit(solution)/shard_map/ppermute | solution.py:15
  62.6 20.6 %copy-start.5 = (u32[32]{0:T(128)S(1)}, u32[32]{0:T(128)}, u32[]{:S(2)}) copy-start(u32[32]{0:T(128)} %constant.159) | copy-start | bytes 388
  63.4 16.1 %collective-permute-start.2 = (bf16[128,1664]{1,0:T(8,128)(2,1)S(1)}, bf16[128,1664]{1,0:T(8,128)(2,1)S(1)}, u32[]{:S(2)}, u32[]{:S(2)}) collective-permute-start(bf16[128,1664]{1,0:T(8,128)(2,1)S(1)} %collective-permute-done), channel_id=1, source_target_pairs={{28,0},{0,4},{4,8},{8,12},{12,16},{16,20},{20,24},{24,28},{29,1},{... | collective-permute-start | bytes 1277960 | tf_op jit(solution)/shard_map/while/body/eval_jaxpr/ppermute | solution.py:15
  67.4 66.3 %copy-start.4 = (u32[32]{0:T(128)S(1)}, u32[32]{0:T(128)}, u32[]{:S(2)}) copy-start(u32[32]{0:T(128)} %constant.143) | copy-start | bytes 388
  79.5 0.8 copy-start.3
Sparse Core Ops, SparseCore 0:
  52.6 18.9 reduce-scatter.1
  83.2 38.9 all-reduce.8
